TPU v7x, 32 devices: a whole 2x2x4 slice. The times are simulated.
32 devices in a mesh: dp: 2 (over y), seq: 16 (over z, x, core).
Axes of the slice: x: 2, y: 2, z: 4, core: 2. Of those that a mesh axis runs over, the one named last changes fastest.
Arguments:
- hidden_in: bfloat16 [2, 1024, 2048], P('dp', 'seq'), may hold values from -6 to 6
- attn_gain: float32 [2048], replicated, may hold values from 0.1 to 1.9
- w_query: bfloat16 [2048, 1280], P('dp'), may hold values from -2 to 2
- w_keyval: bfloat16 [2048, 512], P('dp'), may hold values from -1 to 1
- w_output: bfloat16 [1280, 2048], P(None, 'dp'), may hold values from -0.15625 to 0.15625
- post_gain: float32 [2048], replicated, may hold values from 0.1 to 1.9
Outputs:
- hidden_out: bfloat16 [2, 1024, 2048], P('dp', 'seq')
All inputs are finite; a program needn't handle non-finite values.
Results may differ from a plain program's by a relative error of at most 0.009.
Values may be sent and summed in bfloat16 or wider, within the bound.
No kernel may reach another device: no remote copies, remote signals or barrier semaphores. Data moves between devices by JAX's collectives and lax.ppermute only.
A program may use at most 64 MiB of HBM per device.

v0:
```python
import jax
import jax.numpy as jnp
from jax import lax
from jax.sharding import PartitionSpec as P


def rms_norm(v, gain):
    v = v.astype(jnp.float32)
    return v * lax.rsqrt(jnp.mean(v * v, axis=-1, keepdims=True) + 1e-06) * gain


def rotary(t, positions):
    half = t.shape[-1] // 2
    freq = jnp.exp(-jnp.log(10000.0) * jnp.arange(half, dtype=jnp.float32) * 2.0 / t.shape[-1])
    angle = positions.astype(jnp.float32)[:, None, None] * freq[None, None, :]
    cosine = jnp.cos(angle)
    sine = jnp.sin(angle)
    first = t[..., :half]
    second = t[..., half:]
    return jnp.concatenate(
        [first * cosine - second * sine, second * cosine + first * sine], axis=-1
    )


def local(hidden_in, attn_gain, w_query, w_keyval, w_output, post_gain):
    frame = hidden_in[0]
    count = frame.shape[0]
    head_dim = w_keyval.shape[1] // 2
    width_q = w_query.shape[1]
    num_heads = width_q // head_dim
    normed = rms_norm(frame, attn_gain).astype(jnp.bfloat16)
    slices = lax.all_to_all(normed, "dp", split_axis=1, concat_axis=0, tiled=True)
    joined = jnp.concatenate([w_query, w_keyval], axis=1)
    summed = lax.psum_scatter(
        jnp.dot(slices, joined, preferred_element_type=jnp.float32),
        "dp",
        scatter_dimension=0,
        tiled=True,
    )
    query_raw = summed[:, :width_q]
    keyval_raw = summed[:, width_q:]
    positions = lax.axis_index("seq") * count + jnp.arange(count, dtype=jnp.int32)
    query = (
        rotary(query_raw.reshape(count, num_heads, head_dim), positions) * head_dim ** (-0.5)
    ).astype(jnp.bfloat16)
    keys = rotary(keyval_raw[:, None, :head_dim], positions)[:, 0, :].astype(jnp.bfloat16)
    values = keyval_raw[:, head_dim:].astype(jnp.bfloat16)
    stacked = jnp.transpose(query, (1, 0, 2)).reshape(num_heads * count, head_dim)
    rows_all = num_heads * count
    running_max = jnp.full((rows_all,), -1e30, jnp.float32)
    key_piece = lax.all_gather(keys, "seq", axis=0, tiled=True)
    value_piece = lax.all_gather(values, "seq", axis=0, tiled=True)
    scores = lax.dot_general(
        stacked, key_piece, (((1,), (1,)), ((), ())), preferred_element_type=jnp.float32
    )
    new_max = jnp.maximum(running_max, jnp.max(scores, axis=1))
    expo = jnp.exp(scores - new_max[:, None])
    new_total = jnp.sum(expo, axis=1)
    new_sum = jnp.dot(expo.astype(jnp.bfloat16), value_piece, preferred_element_type=jnp.float32)
    heads = (new_sum / new_total[:, None]).reshape(num_heads, count, head_dim)
    attended = jnp.transpose(heads, (1, 0, 2)).reshape(count, width_q).astype(jnp.bfloat16)
    episode_parts = jnp.dot(
        lax.all_gather(attended, "dp", axis=0, tiled=True),
        w_output,
        preferred_element_type=jnp.float32,
    )
    projected = lax.all_to_all(
        episode_parts.astype(jnp.bfloat16), "dp", split_axis=0, concat_axis=1, tiled=True
    ).astype(episode_parts.dtype)
    result = frame.astype(jnp.float32) + rms_norm(projected, post_gain)
    return result.astype(jnp.bfloat16)[None]


def solution(mesh):
    in_specs = (P("dp", "seq", None), P(), P("dp", None), P("dp", None), P(None, "dp"), P())
    out_specs = P("dp", "seq", None)
    return jax.shard_map(local, mesh=mesh, in_specs=in_specs, out_specs=out_specs, check_vma=False)
```

profile of v0, /device:TPU:0, one launch (start us, length us, event | category | flops | bytes accessed | tf_op | source)
XLA Modules:
  0.0 116.7 jit_solution(12723673413298586071)
XLA Ops:
  6.5 0.0 copy-start
  6.5 1.6 %reshape.228 = f32[64,2,1024]{2,1,0:T(2,128)S(1)} reshape(bf16[1,64,2048]{2,1,0:T(8,128)(2,1)} %param.6) | data formatting | bytes 786432 | tf_op jit(solution)/shard_map/convert_element_type | solution.py:70
  8.2 1.1 multiply_reduce_fusion
  9.3 0.7 mul.156
  10.0 0.3 multiply_convert_fusion
  10.4 9.2 %all_to_all.29 = bf16[64,2,1024]{2,0,1:T(8,128)(2,1)S(1)} all-to-all(bf16[64,2,1024]{2,0,1:T(8,128)(2,1)S(1)} %copy.15), channel_id=1, replica_groups=mesh['dp'=2,'seq'=16] {'dp'}, dimensions={1} | all-to-all | bytes 524288 | tf_op jit(solution)/shard_map/all_to_all | solution.py:32
  19.6 3.7 %fusion = f32[128,1792]{1,0:T(8,128)} fusion(bf16[128,1024]{1,0:T(8,128)(2,1)S(1)} %bitcast.30, bf16[1024,512]{1,0:T(8,128)(2,1)} %param.9, bf16[1024,1280]{1,0:T(8,128)(2,1)} %param.8), kind=kOutput, calls=%fused_computation | convolution fusion | flops 477102080 | bytes 4849664 | tf_op jit(solution)/shard_map/dot_general | solution.py:35
  23.3 0.0 reduce-scatter.2.cloned.1.call-update
  23.3 0.2 multiply_cosine_fusion.1
  23.5 19.2 %reduce-scatter.2.cloned.1.call-done = f32[64,1792]{1,0:T(8,128)} async-done(((f32[128,1792]{1,0:T(8,128)}), f32[64,1792]{1,0:T(8,128)}) %reduce-scatter.2.cloned.1.call-update) | async-done | bytes 458768 | tf_op jit(solution)/shard_map/reduce_scatter | solution.py:34
  42.7 1.0 slice.32
  43.7 0.1 reshape.226
  43.8 0.1 multiply_subtract_fusion
  43.9 0.1 fusion.13
  44.0 0.8 slice_bitcast_fusion
  44.9 0.2 fusion.19
  45.1 22.9 %all-gather = bf16[1024,1,256]{2,0,1:T(8,128)(2,1)S(1)} all-gather(bf16[64,1,256]{2,0,1:T(8,128)(2,1)S(1)} %pad_maximum_fusion), channel_id=2, replica_groups=mesh['dp'=2,'seq'=16] {'seq'}, dimensions={0}, use_global_device_ids=true | all-gather | bytes 557056 | tf_op jit(solution)/shard_map/all_gather | solution.py:51
  68.0 0.5 fusion.23
  68.4 0.8 slice.49
  69.3 18.9 %all_gather.10 = bf16[1024,256]{1,0:T(8,128)(2,1)S(1)} all-gather(bf16[64,256]{1,0:T(8,128)(2,1)S(1)} %slice.49), channel_id=1, replica_groups=mesh['dp'=2,'seq'=16] {'seq'}, dimensions={0}, use_global_device_ids=true | all-gather | bytes 557056 | tf_op jit(solution)/shard_map/all_gather | solution.py:52
  88.1 0.4 fusion.5
  88.5 0.4 fusion.4
  88.9 7.1 %all_gather.11 = bf16[128,1280]{1,0:T(8,128)(2,1)S(1)} all-gather(bf16[64,1280]{1,0:T(8,128)(2,1)S(1)} %bitcast.29), channel_id=1, replica_groups=mesh['dp'=2,'seq'=16] {'dp'}, dimensions={0}, use_global_device_ids=true | all-gather | bytes 491520 | tf_op jit(solution)/shard_map/all_gather | solution.py:63
  96.0 0.5 convolution_convert_fusion
  96.5 0.0 copy-start.1
  96.6 0.0 copy-start.2
  96.6 7.7 %all_to_all.30 = bf16[2,64,1024]{2,1,0:T(8,128)(2,1)S(1)} all-to-all(bf16[2,64,1024]{2,1,0:T(8,128)(2,1)S(1)} %bitcast.27), channel_id=1, replica_groups=mesh['dp'=2,'seq'=16] {'dp'}, dimensions={0} | all-to-all | bytes 524288 | tf_op jit(solution)/shard_map/all_to_all | solution.py:67
  104.3 1.2 %copy.18 = f32[64,2,1024]{2,1,0:T(2,128)} copy(f32[64,2,1024]{2,0,1:T(8,128)S(1)} %convert_bitcast_fusion) | data formatting | bytes 1048576 | tf_op jit(solution)/shard_map/convert_element_type | solution.py:69
  105.5 2.3 %reshape.229 = f32[1,64,2048]{2,1,0:T(8,128)} reshape(f32[64,2,1024]{2,1,0:T(2,128)} %copy.18) | data formatting | bytes 1048576 | tf_op jit(solution)/shard_map/convert_element_type | solution.py:69
  107.8 0.2 fusion.9
  108.0 0.0 copy-done.2
  108.0 1.9 %add_convert_fusion = bf16[1,64,2048]{2,1,0:T(8,128)(2,1)} fusion(f32[1,64,2048]{2,1,0:T(8,128)} %reshape.229, f32[2048]{0:T(1024)S(1)} %copy-done.2, f32[64]{0:T(128)S(1)} %add_rsqrt_fusion, bf16[1,64,2048]{2,1,0:T(8,128)(2,1)S(1)} %copy-done.1), kind=kLoop, calls=%fused_computation.18 | loop fusion | flops 655360 | bytes 1057024 | tf_op jit(solution)/shard_map/convert_element_type | solution.py:71
  (13 shorter events, 0.2 us)
Async XLA Ops:
  6.5 89.5 %copy-start = (bf16[1280,1024]{1,0:T(8,128)(2,1)S(1)}, bf16[1280,1024]{1,0:T(8,128)(2,1)}, u32[]{:S(2)}) copy-start(bf16[1280,1024]{1,0:T(8,128)(2,1)} %param.10) | copy-start | bytes 7864324
  6.5 36.2 %reduce-scatter.2.cloned.1.call-start = ((), (), s32[]{:S(2)}) async-start(), calls=%async_computation.3 | async-start | bytes 1376256 | tf_op jit(solution)/shard_map/reduce_scatter | solution.py:34
  96.5 11.4 %copy-start.1 = (bf16[1,64,2048]{2,1,0:T(8,128)(2,1)S(1)}, bf16[1,64,2048]{2,1,0:T(8,128)(2,1)}, u32[]{:S(2)}) copy-start(bf16[1,64,2048]{2,1,0:T(8,128)(2,1)} %param.6) | copy-start | bytes 786436
  96.6 11.4 %copy-start.2 = (f32[2048]{0:T(1024)S(1)}, f32[2048]{0:T(1024)}, u32[]{:S(2)}) copy-start(f32[2048]{0:T(1024)} %param.11) | copy-start | bytes 24580
Sparse Core Ops, SparseCore 0:
  23.4 19.2 reduce-scatter.1
where the time goes:
time: 117 us
  blocking collectives  65.8 us (56%)
  waiting for transfers between devices  19.2 us (16%)
  between operations  13.6 us (12%)
  local copies, waits for them, and re-layouts  8.72 us (7%)
  matrix products  5.02 us (4%)
  other arithmetic  4.41 us (4%)
    all_gather x1, blocking collectives, local(): key_piece = lax.all_gather(keys, 'seq', axis=0, tiled=True)  22.9 us
    reduce_scatter x1, waiting for transfers between devices, local(): lax.psum_scatter(jnp.dot(slices, joined, preferred_element_type=jnp.float...  19.2 us
    all_gather x1, blocking collectives, local(): value_piece = lax.all_gather(values, 'seq', axis=0, tiled=True)  18.9 us
    all_to_all x1, blocking collectives, local(): lax.all_to_all(normed, 'dp', split_axis=1, concat_axis=0, tiled=True)  9.24 us
    all_to_all x1, blocking collectives, local(): lax.all_to_all(episode_parts.astype(jnp.bfloat16), 'dp', split_axis=0, co...  7.69 us
    all_gather x1, blocking collectives, local(): lax.all_gather(attended, 'dp', axis=0, tiled=True)  7.11 us
    dot_general x1, matrix products, local(): jnp.dot(slices, joined, preferred_element_type=jnp.float32)  3.65 us
    convert_element_type x2, local copies, waits for them, and re-layouts, local(): projected = lax.all_to_all(episode_parts.astype(jnp.bfloat16), 'dp', spli...  3.5 us
  transfers between devices with their start and end apart: 1, of which 1 were waited for; matrix products, arithmetic and copies ran while one was open for 0% of the time, Pallas kernels for 0%

commit v1 on v0

--- a/solution.py
+++ b/solution.py
@@ -48,7 +48,12 @@
     stacked = jnp.transpose(query, (1, 0, 2)).reshape(num_heads * count, head_dim)
     rows_all = num_heads * count
     running_max = jnp.full((rows_all,), -1e30, jnp.float32)
-    key_piece = lax.all_gather(keys, "seq", axis=0, tiled=True)
+    ring = [keys]
+    for hop in range(15):
+        ring.append(lax.ppermute(ring[-1], "seq", [(dev, (dev + 1) % 16) for dev in range(16)]))
+    key_piece = jnp.roll(
+        jnp.concatenate(ring[::-1], axis=0), (lax.axis_index("seq") + 1) * ring[0].shape[0], axis=0
+    )
     value_piece = lax.all_gather(values, "seq", axis=0, tiled=True)
     scores = lax.dot_general(
         stacked, key_piece, (((1,), (1,)), ((), ())), preferred_element_type=jnp.float32

time: 117 us -> 184 us (1.57)
  waiting for transfers between devices: 19.2 us -> 101 us
  blocking collectives: 65.8 us -> 43.8 us
  local copies, waits for them, and re-layouts: 8.72 us -> 12.8 us
    ppermute x0 -> x15, waiting for transfers between devices: none -> 82 us  [local(): lax.ppermute(ring[-1], 'seq', [(dev, (dev + 1) % 16) for dev in range(16)])]
    all_gather x1 -> x0, blocking collectives: 22.9 us -> none  [local(): key_piece = lax.all_gather(keys, 'seq', axis=0, tiled=True)]
    unnamed x7 -> x83, local copies, waits for them, and re-layouts: 0.03 us -> 4.09 us
    all_gather x1, blocking collectives: 18.9 us -> 20.8 us  [local(): value_piece = lax.all_gather(values, 'seq', axis=0, tiled=True)]
  transfers between devices with their start and end apart: 1 -> 16, of which waited for: 1 -> 15; matrix products, arithmetic and copies ran while one was open for 0% -> 2% of each run, Pallas kernels for 0% -> 0%
where the time goes in v1:
time: 184 us; the launch traced here: 183 us
  waiting for transfers between devices  101 us (55%)
  blocking collectives  43.8 us (24%)
  between operations  14 us (8%)
  local copies, waits for them, and re-layouts  12.8 us (7%)
  other arithmetic  5.81 us (3%)
  matrix products  5.04 us (3%)
    ppermute x15, waiting for transfers between devices, local(): lax.ppermute(ring[-1], 'seq', [(dev, (dev + 1) % 16) for dev in range(16)])  82 us
    all_gather x1, blocking collectives, local(): value_piece = lax.all_gather(values, 'seq', axis=0, tiled=True)  20.8 us
    reduce_scatter x1, waiting for transfers between devices, local(): lax.psum_scatter(jnp.dot(slices, joined, preferred_element_type=jnp.float...  19.4 us
    all_to_all x1, blocking collectives, local(): lax.all_to_all(normed, 'dp', split_axis=1, concat_axis=0, tiled=True)  9.24 us
    all_to_all x1, blocking collectives, local(): lax.all_to_all(episode_parts.astype(jnp.bfloat16), 'dp', split_axis=0, co...  7.69 us
    all_gather x1, blocking collectives, local(): lax.all_gather(attended, 'dp', axis=0, tiled=True)  6.1 us
    unnamed x83, local copies, waits for them, and re-layouts  4.09 us
  transfers between devices with their start and end apart: 16, of which 15 were waited for; matrix products, arithmetic and copies ran while one was open for 2% of the time, Pallas kernels for 0%

profile of v1, /device:TPU:0, one launch (start us, length us, event | category | flops | bytes accessed | tf_op | source)
XLA Modules:
  0.0 183.3 jit_solution(122346253841614144)
XLA Ops:
  6.5 1.6 reshape.228
  8.2 1.1 multiply_reduce_fusion
  10.4 9.2 %all_to_all.29 = bf16[64,2,1024]{2,0,1:T(8,128)(2,1)S(1)} all-to-all(bf16[64,2,1024]{2,0,1:T(8,128)(2,1)S(1)} %copy.15), channel_id=1, replica_groups=mesh['dp'=2,'seq'=16] {'dp'}, dimensions={1} | all-to-all | bytes 524288 | tf_op jit(solution)/shard_map/all_to_all | solution.py:32
  19.6 3.7 %fusion = f32[128,1792]{1,0:T(8,128)} fusion(bf16[128,1024]{1,0:T(8,128)(2,1)S(1)} %bitcast.31, bf16[1024,512]{1,0:T(8,128)(2,1)} %param.9, bf16[1024,1280]{1,0:T(8,128)(2,1)} %param.8), kind=kOutput, calls=%fused_computation | convolution fusion | flops 477102080 | bytes 4849664 | tf_op jit(solution)/shard_map/dot_general | solution.py:35
  23.3 19.4 %reduce-scatter.2.cloned.1.call-done = f32[64,1792]{1,0:T(8,128)} async-done(((f32[128,1792]{1,0:T(8,128)}), f32[64,1792]{1,0:T(8,128)}) %reduce-scatter.2.cloned.1.call-update) | async-done | bytes 458768 | tf_op jit(solution)/shard_map/reduce_scatter | solution.py:34
  42.8 0.8 slice_bitcast_fusion
  43.9 6.0 %collective-permute-done = bf16[64,256]{1,0:T(8,128)(2,1)S(1)} collective-permute-done((bf16[64,256]{1,0:T(8,128)(2,1)S(1)}, bf16[64,256]{1,0:T(8,128)(2,1)S(1)}, u32[]{:S(2)}, u32[]{:S(2)}) %collective-permute-start) | collective-permute-done | bytes 32800 | tf_op jit(solution)/shard_map/ppermute | solution.py:53
  49.9 6.0 %collective-permute-done.1 = bf16[64,256]{1,0:T(8,128)(2,1)S(1)} collective-permute-done((bf16[64,256]{1,0:T(8,128)(2,1)S(1)}, bf16[64,256]{1,0:T(8,128)(2,1)S(1)}, u32[]{:S(2)}, u32[]{:S(2)}) %collective-permute-start.1) | collective-permute-done | bytes 32800 | tf_op jit(solution)/shard_map/ppermute | solution.py:53
  56.0 6.0 %collective-permute-done.2 = bf16[64,256]{1,0:T(8,128)(2,1)S(1)} collective-permute-done((bf16[64,256]{1,0:T(8,128)(2,1)S(1)}, bf16[64,256]{1,0:T(8,128)(2,1)S(1)}, u32[]{:S(2)}, u32[]{:S(2)}) %collective-permute-start.2) | collective-permute-done | bytes 32800 | tf_op jit(solution)/shard_map/ppermute | solution.py:53
  62.0 6.0 %collective-permute-done.3 = bf16[64,256]{1,0:T(8,128)(2,1)S(1)} collective-permute-done((bf16[64,256]{1,0:T(8,128)(2,1)S(1)}, bf16[64,256]{1,0:T(8,128)(2,1)S(1)}, u32[]{:S(2)}, u32[]{:S(2)}) %collective-permute-start.3) | collective-permute-done | bytes 32800 | tf_op jit(solution)/shard_map/ppermute | solution.py:53
  68.0 6.0 %collective-permute-done.4 = bf16[64,256]{1,0:T(8,128)(2,1)S(1)} collective-permute-done((bf16[64,256]{1,0:T(8,128)(2,1)S(1)}, bf16[64,256]{1,0:T(8,128)(2,1)S(1)}, u32[]{:S(2)}, u32[]{:S(2)}) %collective-permute-start.4) | collective-permute-done | bytes 32800 | tf_op jit(solution)/shard_map/ppermute | solution.py:53
  74.1 6.0 %collective-permute-done.5 = bf16[64,256]{1,0:T(8,128)(2,1)S(1)} collective-permute-done((bf16[64,256]{1,0:T(8,128)(2,1)S(1)}, bf16[64,256]{1,0:T(8,128)(2,1)S(1)}, u32[]{:S(2)}, u32[]{:S(2)}) %collective-permute-start.5) | collective-permute-done | bytes 32800 | tf_op jit(solution)/shard_map/ppermute | solution.py:53
  80.1 6.0 %collective-permute-done.6 = bf16[64,256]{1,0:T(8,128)(2,1)S(1)} collective-permute-done((bf16[64,256]{1,0:T(8,128)(2,1)S(1)}, bf16[64,256]{1,0:T(8,128)(2,1)S(1)}, u32[]{:S(2)}, u32[]{:S(2)}) %collective-permute-start.6) | collective-permute-done | bytes 32800 | tf_op jit(solution)/shard_map/ppermute | solution.py:53
  86.1 6.0 %collective-permute-done.7 = bf16[64,256]{1,0:T(8,128)(2,1)S(1)} collective-permute-done((bf16[64,256]{1,0:T(8,128)(2,1)S(1)}, bf16[64,256]{1,0:T(8,128)(2,1)S(1)}, u32[]{:S(2)}, u32[]{:S(2)}) %collective-permute-start.7) | collective-permute-done | bytes 32800 | tf_op jit(solution)/shard_map/ppermute | solution.py:53
  92.2 6.0 %collective-permute-done.8 = bf16[64,256]{1,0:T(8,128)(2,1)S(1)} collective-permute-done((bf16[64,256]{1,0:T(8,128)(2,1)S(1)}, bf16[64,256]{1,0:T(8,128)(2,1)S(1)}, u32[]{:S(2)}, u32[]{:S(2)}) %collective-permute-start.8) | collective-permute-done | bytes 32800 | tf_op jit(solution)/shard_map/ppermute | solution.py:53
  98.2 6.0 %collective-permute-done.9 = bf16[64,256]{1,0:T(8,128)(2,1)S(1)} collective-permute-done((bf16[64,256]{1,0:T(8,128)(2,1)S(1)}, bf16[64,256]{1,0:T(8,128)(2,1)S(1)}, u32[]{:S(2)}, u32[]{:S(2)}) %collective-permute-start.9) | collective-permute-done | bytes 32800 | tf_op jit(solution)/shard_map/ppermute | solution.py:53
  104.3 6.0 %collective-permute-done.10 = bf16[64,256]{1,0:T(8,128)(2,1)S(1)} collective-permute-done((bf16[64,256]{1,0:T(8,128)(2,1)S(1)}, bf16[64,256]{1,0:T(8,128)(2,1)S(1)}, u32[]{:S(2)}, u32[]{:S(2)}) %collective-permute-start.10) | collective-permute-done | bytes 32800 | tf_op jit(solution)/shard_map/ppermute | solution.py:53
  110.5 0.8 multiply_cosine_fusion.1
  111.3 0.8 slice.49
  112.1 4.5 %collective-permute-done.11 = bf16[64,256]{1,0:T(8,128)(2,1)} collective-permute-done((bf16[64,256]{1,0:T(8,128)(2,1)S(1)}, bf16[64,256]{1,0:T(8,128)(2,1)}, u32[]{:S(2)}, u32[]{:S(2)}) %collective-permute-start.11) | collective-permute-done | bytes 32800 | tf_op jit(solution)/shard_map/ppermute | solution.py:53
  116.6 20.8 %all_gather.6 = bf16[1024,256]{1,0:T(8,128)(2,1)} all-gather(bf16[64,256]{1,0:T(8,128)(2,1)S(1)} %slice.49), channel_id=1, replica_groups=mesh['dp'=2,'seq'=16] {'seq'}, dimensions={0}, use_global_device_ids=true | all-gather | bytes 557056 | tf_op jit(solution)/shard_map/all_gather | solution.py:57
  137.4 1.0 slice.32
  138.8 0.8 multiply_subtract_fusion
  139.7 5.3 %collective-permute-done.13 = bf16[64,256]{1,0:T(8,128)(2,1)S(1)} collective-permute-done((bf16[64,256]{1,0:T(8,128)(2,1)}, bf16[64,256]{1,0:T(8,128)(2,1)S(1)}, u32[]{:S(2)}, u32[]{:S(2)}) %collective-permute-start.13) | collective-permute-done | bytes 32800 | tf_op jit(solution)/shard_map/ppermute | solution.py:53
  145.0 5.9 %collective-permute-done.14 = bf16[64,256]{1,0:T(8,128)(2,1)S(1)} collective-permute-done((bf16[64,256]{1,0:T(8,128)(2,1)S(1)}, bf16[64,256]{1,0:T(8,128)(2,1)S(1)}, u32[]{:S(2)}, u32[]{:S(2)}) %collective-permute-start.14) | collective-permute-done | bytes 32800 | tf_op jit(solution)/shard_map/ppermute | solution.py:53
  151.7 0.8 constant_dynamic-update-slice_fusion.28
  153.6 0.8 constant_dynamic-update-slice_fusion.13
  156.5 6.1 %all_gather.7 = bf16[128,1280]{1,0:T(8,128)(2,1)S(1)} all-gather(bf16[64,1280]{1,0:T(8,128)(2,1)S(1)} %bitcast.29), channel_id=1, replica_groups=mesh['dp'=2,'seq'=16] {'dp'}, dimensions={0}, use_global_device_ids=true | all-gather | bytes 491520 | tf_op jit(solution)/shard_map/all_gather | solution.py:68
  163.2 7.7 %all_to_all.30 = bf16[2,64,1024]{2,1,0:T(8,128)(2,1)S(1)} all-to-all(bf16[2,64,1024]{2,1,0:T(8,128)(2,1)S(1)} %bitcast.28), channel_id=1, replica_groups=mesh['dp'=2,'seq'=16] {'dp'}, dimensions={0} | all-to-all | bytes 524288 | tf_op jit(solution)/shard_map/all_to_all | solution.py:72
  170.9 1.2 copy.18
  172.1 2.3 %reshape.229 = f32[1,64,2048]{2,1,0:T(8,128)} reshape(f32[64,2,1024]{2,1,0:T(2,128)} %copy.18) | data formatting | bytes 1048576 | tf_op jit(solution)/shard_map/convert_element_type | solution.py:74
  174.6 1.9 %add_convert_fusion = bf16[1,64,2048]{2,1,0:T(8,128)(2,1)} fusion(f32[1,64,2048]{2,1,0:T(8,128)} %reshape.229, f32[2048]{0:T(1024)S(1)} %copy-done.25, f32[64]{0:T(128)S(1)} %add_rsqrt_fusion, bf16[1,64,2048]{2,1,0:T(8,128)(2,1)S(1)} %copy-done.1), kind=kLoop, calls=%fused_computation.16 | loop fusion | flops 655360 | bytes 1057024 | tf_op jit(solution)/shard_map/convert_element_type | solution.py:76
  (120 shorter events, 6.4 us)
Async XLA Ops:
  6.5 156.1 %copy-start = (bf16[1280,1024]{1,0:T(8,128)(2,1)S(1)}, bf16[1280,1024]{1,0:T(8,128)(2,1)}, u32[]{:S(2)}) copy-start(bf16[1280,1024]{1,0:T(8,128)(2,1)} %param.10) | copy-start | bytes 7864324
  6.5 36.2 %reduce-scatter.2.cloned.1.call-start = ((), (), s32[]{:S(2)}) async-start(), calls=%async_computation.3 | async-start | bytes 1376256 | tf_op jit(solution)/shard_map/reduce_scatter | solution.py:34
  43.8 6.1 %collective-permute-start = (bf16[64,256]{1,0:T(8,128)(2,1)S(1)}, bf16[64,256]{1,0:T(8,128)(2,1)S(1)}, u32[]{:S(2)}, u32[]{:S(2)}) collective-permute-start(bf16[64,256]{1,0:T(8,128)(2,1)S(1)} %maximum_bitcast_fusion), channel_id=1, source_target_pairs={{0,1},{1,2},{2,3},{3,4},{4,5},{5,6},{6,7},{7,8},{8,9},{9,10},{10,1... | collective-permute-start | bytes 98312 | tf_op jit(solution)/shard_map/ppermute | solution.py:53
  49.9 60.4 %copy-start.3 = (bf16[64,256]{1,0:T(8,128)(2,1)}, bf16[64,256]{1,0:T(8,128)(2,1)S(1)}, u32[]{:S(2)}) copy-start(bf16[64,256]{1,0:T(8,128)(2,1)S(1)} %collective-permute-done) | copy-start | bytes 98308
  49.9 6.0 %collective-permute-start.1 = (bf16[64,256]{1,0:T(8,128)(2,1)S(1)}, bf16[64,256]{1,0:T(8,128)(2,1)S(1)}, u32[]{:S(2)}, u32[]{:S(2)}) collective-permute-start(bf16[64,256]{1,0:T(8,128)(2,1)S(1)} %collective-permute-done), channel_id=1, source_target_pairs={{0,1},{1,2},{2,3},{3,4},{4,5},{5,6},{6,7},{7,8},{8,9},{9,10},{10,1... | collective-permute-start | bytes 98312 | tf_op jit(solution)/shard_map/ppermute | solution.py:53
  55.9 54.4 %copy-start.5 = (bf16[64,256]{1,0:T(8,128)(2,1)}, bf16[64,256]{1,0:T(8,128)(2,1)S(1)}, u32[]{:S(2)}) copy-start(bf16[64,256]{1,0:T(8,128)(2,1)S(1)} %collective-permute-done.1) | copy-start | bytes 98308
  55.9 6.0 %collective-permute-start.2 = (bf16[64,256]{1,0:T(8,128)(2,1)S(1)}, bf16[64,256]{1,0:T(8,128)(2,1)S(1)}, u32[]{:S(2)}, u32[]{:S(2)}) collective-permute-start(bf16[64,256]{1,0:T(8,128)(2,1)S(1)} %collective-permute-done.1), channel_id=1, source_target_pairs={{0,1},{1,2},{2,3},{3,4},{4,5},{5,6},{6,7},{7,8},{8,9},{9,10},{10,1... | collective-permute-start | bytes 98312 | tf_op jit(solution)/shard_map/ppermute | solution.py:53
  62.0 48.3 %copy-start.7 = (bf16[64,256]{1,0:T(8,128)(2,1)}, bf16[64,256]{1,0:T(8,128)(2,1)S(1)}, u32[]{:S(2)}) copy-start(bf16[64,256]{1,0:T(8,128)(2,1)S(1)} %collective-permute-done.2) | copy-start | bytes 98308
  62.0 6.0 %collective-permute-start.3 = (bf16[64,256]{1,0:T(8,128)(2,1)S(1)}, bf16[64,256]{1,0:T(8,128)(2,1)S(1)}, u32[]{:S(2)}, u32[]{:S(2)}) collective-permute-start(bf16[64,256]{1,0:T(8,128)(2,1)S(1)} %collective-permute-done.2), channel_id=1, source_target_pairs={{0,1},{1,2},{2,3},{3,4},{4,5},{5,6},{6,7},{7,8},{8,9},{9,10},{10,1... | collective-permute-start | bytes 98312 | tf_op jit(solution)/shard_map/ppermute | solution.py:53
  68.0 42.3 %copy-start.9 = (bf16[64,256]{1,0:T(8,128)(2,1)}, bf16[64,256]{1,0:T(8,128)(2,1)S(1)}, u32[]{:S(2)}) copy-start(bf16[64,256]{1,0:T(8,128)(2,1)S(1)} %collective-permute-done.3) | copy-start | bytes 98308
  68.0 6.0 %collective-permute-start.4 = (bf16[64,256]{1,0:T(8,128)(2,1)S(1)}, bf16[64,256]{1,0:T(8,128)(2,1)S(1)}, u32[]{:S(2)}, u32[]{:S(2)}) collective-permute-start(bf16[64,256]{1,0:T(8,128)(2,1)S(1)} %collective-permute-done.3), channel_id=1, source_target_pairs={{0,1},{1,2},{2,3},{3,4},{4,5},{5,6},{6,7},{7,8},{8,9},{9,10},{10,1... | collective-permute-start | bytes 98312 | tf_op jit(solution)/shard_map/ppermute | solution.py:53
  74.1 36.3 %copy-start.11 = (bf16[64,256]{1,0:T(8,128)(2,1)}, bf16[64,256]{1,0:T(8,128)(2,1)S(1)}, u32[]{:S(2)}) copy-start(bf16[64,256]{1,0:T(8,128)(2,1)S(1)} %collective-permute-done.4) | copy-start | bytes 98308
  74.1 6.0 %collective-permute-start.5 = (bf16[64,256]{1,0:T(8,128)(2,1)S(1)}, bf16[64,256]{1,0:T(8,128)(2,1)S(1)}, u32[]{:S(2)}, u32[]{:S(2)}) collective-permute-start(bf16[64,256]{1,0:T(8,128)(2,1)S(1)} %collective-permute-done.4), channel_id=1, source_target_pairs={{0,1},{1,2},{2,3},{3,4},{4,5},{5,6},{6,7},{7,8},{8,9},{9,10},{10,1... | collective-permute-start | bytes 98312 | tf_op jit(solution)/shard_map/ppermute | solution.py:53
  80.1 30.2 %copy-start.13 = (bf16[64,256]{1,0:T(8,128)(2,1)}, bf16[64,256]{1,0:T(8,128)(2,1)S(1)}, u32[]{:S(2)}) copy-start(bf16[64,256]{1,0:T(8,128)(2,1)S(1)} %collective-permute-done.5) | copy-start | bytes 98308
  80.1 6.0 %collective-permute-start.6 = (bf16[64,256]{1,0:T(8,128)(2,1)S(1)}, bf16[64,256]{1,0:T(8,128)(2,1)S(1)}, u32[]{:S(2)}, u32[]{:S(2)}) collective-permute-start(bf16[64,256]{1,0:T(8,128)(2,1)S(1)} %collective-permute-done.5), channel_id=1, source_target_pairs={{0,1},{1,2},{2,3},{3,4},{4,5},{5,6},{6,7},{7,8},{8,9},{9,10},{10,1... | collective-permute-start | bytes 98312 | tf_op jit(solution)/shard_map/ppermute | solution.py:53
  86.1 24.2 %copy-start.15 = (bf16[64,256]{1,0:T(8,128)(2,1)}, bf16[64,256]{1,0:T(8,128)(2,1)S(1)}, u32[]{:S(2)}) copy-start(bf16[64,256]{1,0:T(8,128)(2,1)S(1)} %collective-permute-done.6) | copy-start | bytes 98308
  86.1 6.0 %collective-permute-start.7 = (bf16[64,256]{1,0:T(8,128)(2,1)S(1)}, bf16[64,256]{1,0:T(8,128)(2,1)S(1)}, u32[]{:S(2)}, u32[]{:S(2)}) collective-permute-start(bf16[64,256]{1,0:T(8,128)(2,1)S(1)} %collective-permute-done.6), channel_id=1, source_target_pairs={{0,1},{1,2},{2,3},{3,4},{4,5},{5,6},{6,7},{7,8},{8,9},{9,10},{10,1... | collective-permute-start | bytes 98312 | tf_op jit(solution)/shard_map/ppermute | solution.py:53
  92.2 18.2 %copy-start.17 = (bf16[64,256]{1,0:T(8,128)(2,1)}, bf16[64,256]{1,0:T(8,128)(2,1)S(1)}, u32[]{:S(2)}) copy-start(bf16[64,256]{1,0:T(8,128)(2,1)S(1)} %collective-permute-done.7) | copy-start | bytes 98308
  92.2 6.0 %collective-permute-start.8 = (bf16[64,256]{1,0:T(8,128)(2,1)S(1)}, bf16[64,256]{1,0:T(8,128)(2,1)S(1)}, u32[]{:S(2)}, u32[]{:S(2)}) collective-permute-start(bf16[64,256]{1,0:T(8,128)(2,1)S(1)} %collective-permute-done.7), channel_id=1, source_target_pairs={{0,1},{1,2},{2,3},{3,4},{4,5},{5,6},{6,7},{7,8},{8,9},{9,10},{10,1... | collective-permute-start | bytes 98312 | tf_op jit(solution)/shard_map/ppermute | solution.py:53
  98.2 6.0 %collective-permute-start.9 = (bf16[64,256]{1,0:T(8,128)(2,1)S(1)}, bf16[64,256]{1,0:T(8,128)(2,1)S(1)}, u32[]{:S(2)}, u32[]{:S(2)}) collective-permute-start(bf16[64,256]{1,0:T(8,128)(2,1)S(1)} %collective-permute-done.8), channel_id=1, source_target_pairs={{0,1},{1,2},{2,3},{3,4},{4,5},{5,6},{6,7},{7,8},{8,9},{9,10},{10,1... | collective-permute-start | bytes 98312 | tf_op jit(solution)/shard_map/ppermute | solution.py:53
  104.3 6.0 %collective-permute-start.10 = (bf16[64,256]{1,0:T(8,128)(2,1)S(1)}, bf16[64,256]{1,0:T(8,128)(2,1)S(1)}, u32[]{:S(2)}, u32[]{:S(2)}) collective-permute-start(bf16[64,256]{1,0:T(8,128)(2,1)S(1)} %collective-permute-done.9), channel_id=1, source_target_pairs={{0,1},{1,2},{2,3},{3,4},{4,5},{5,6},{6,7},{7,8},{8,9},{9,10},{10,1... | collective-permute-start | bytes 98312 | tf_op jit(solution)/shard_map/ppermute | solution.py:53
  110.4 27.0 %copy-start.23 = (bf16[64,256]{1,0:T(8,128)(2,1)}, bf16[64,256]{1,0:T(8,128)(2,1)S(1)}, u32[]{:S(2)}) copy-start(bf16[64,256]{1,0:T(8,128)(2,1)S(1)} %collective-permute-done.10) | copy-start | bytes 98308
  110.4 6.2 %collective-permute-start.11 = (bf16[64,256]{1,0:T(8,128)(2,1)S(1)}, bf16[64,256]{1,0:T(8,128)(2,1)}, u32[]{:S(2)}, u32[]{:S(2)}) collective-permute-start(bf16[64,256]{1,0:T(8,128)(2,1)S(1)} %collective-permute-done.10), channel_id=1, source_target_pairs={{0,1},{1,2},{2,3},{3,4},{4,5},{5,6},{6,7},{7,8},{8,9},{9,10},{10,1... | collective-permute-start | bytes 98312 | tf_op jit(solution)/shard_map/ppermute | solution.py:53
  116.6 22.0 %collective-permute-start.12 = (bf16[64,256]{1,0:T(8,128)(2,1)}, bf16[64,256]{1,0:T(8,128)(2,1)}, u32[]{:S(2)}, u32[]{:S(2)}) collective-permute-start(bf16[64,256]{1,0:T(8,128)(2,1)} %collective-permute-done.11), channel_id=1, source_target_pairs={{0,1},{1,2},{2,3},{3,4},{4,5},{5,6},{6,7},{7,8},{8,9},{9,10},{10,1... | collective-permute-start | bytes 98312 | tf_op jit(solution)/shard_map/ppermute | solution.py:53
  138.6 14.9 %copy-start.12 = (bf16[64,256]{1,0:T(8,128)(2,1)S(1)}, bf16[64,256]{1,0:T(8,128)(2,1)}, u32[]{:S(2)}) copy-start(bf16[64,256]{1,0:T(8,128)(2,1)} %copy-done.11) | copy-start | bytes 98308
  138.6 14.9 %copy-start.10 = (bf16[64,256]{1,0:T(8,128)(2,1)S(1)}, bf16[64,256]{1,0:T(8,128)(2,1)}, u32[]{:S(2)}) copy-start(bf16[64,256]{1,0:T(8,128)(2,1)} %copy-done.9) | copy-start | bytes 98308
  138.6 14.9 %copy-start.8 = (bf16[64,256]{1,0:T(8,128)(2,1)S(1)}, bf16[64,256]{1,0:T(8,128)(2,1)}, u32[]{:S(2)}) copy-start(bf16[64,256]{1,0:T(8,128)(2,1)} %copy-done.7) | copy-start | bytes 98308
  138.6 14.9 %copy-start.6 = (bf16[64,256]{1,0:T(8,128)(2,1)S(1)}, bf16[64,256]{1,0:T(8,128)(2,1)}, u32[]{:S(2)}) copy-start(bf16[64,256]{1,0:T(8,128)(2,1)} %copy-done.5) | copy-start | bytes 98308
  138.6 14.9 %copy-start.4 = (bf16[64,256]{1,0:T(8,128)(2,1)S(1)}, bf16[64,256]{1,0:T(8,128)(2,1)}, u32[]{:S(2)}) copy-start(bf16[64,256]{1,0:T(8,128)(2,1)} %copy-done.3) | copy-start | bytes 98308
  138.6 16.5 %copy-start.24 = (bf16[64,256]{1,0:T(8,128)(2,1)S(1)}, bf16[64,256]{1,0:T(8,128)(2,1)}, u32[]{:S(2)}) copy-start(bf16[64,256]{1,0:T(8,128)(2,1)} %copy-done.23) | copy-start | bytes 98308
  138.6 6.3 %collective-permute-start.13 = (bf16[64,256]{1,0:T(8,128)(2,1)}, bf16[64,256]{1,0:T(8,128)(2,1)S(1)}, u32[]{:S(2)}, u32[]{:S(2)}) collective-permute-start(bf16[64,256]{1,0:T(8,128)(2,1)} %collective-permute-done.12), channel_id=1, source_target_pairs={{0,1},{1,2},{2,3},{3,4},{4,5},{5,6},{6,7},{7,8},{8,9},{9,10},{10,1... | collective-permute-start | bytes 98312 | tf_op jit(solution)/shard_map/ppermute | solution.py:53
  144.9 6.0 %collective-permute-start.14 = (bf16[64,256]{1,0:T(8,128)(2,1)S(1)}, bf16[64,256]{1,0:T(8,128)(2,1)S(1)}, u32[]{:S(2)}, u32[]{:S(2)}) collective-permute-start(bf16[64,256]{1,0:T(8,128)(2,1)S(1)} %collective-permute-done.13), channel_id=1, source_target_pairs={{0,1},{1,2},{2,3},{3,4},{4,5},{5,6},{6,7},{7,8},{8,9},{9,10},{10,1... | collective-permute-start | bytes 98312 | tf_op jit(solution)/shard_map/ppermute | solution.py:53
  (10 other events, 119.6 us)
Sparse Core Ops, SparseCore 0:
  23.4 19.2 reduce-scatter.1
